TPU v7x, 32 devices: a whole 2x2x4 slice. The times are simulated.
32 devices in a mesh: row: 2 (over x), col: 16 (over z, y, core).
Axes of the slice: x: 2, y: 2, z: 4, core: 2. Of those that a mesh axis runs over, the one named last changes fastest.
Arguments:
- matrix: bfloat16 [1024, 65536], P('row', 'col'), may hold values from -0.1875 to 0.1875
- measured: float32 [256, 1024], P(None, 'row'), may hold values from -160 to 160
- support: int32 [4, 1024], replicated, may hold values from 0 to 65535, as said below
Outputs:
- estimate: float32 [256, 65536], P('row', 'col')
- row_norms: float32 [65536], P('col')
- residual_energy: float32 [4], replicated
Inputs may be any that keep to these rules, and one draw needn't show every extreme that they name: Each row of support lists 1024 distinct signal-row indices in increasing order; in every row, each aligned block of 4096 indices (the signal rows of one index of col) holds at most 128 of them, and some block exactly 128.
All inputs are finite; a program needn't handle non-finite values.
Results may differ from a plain program's by a relative error of at most 0.015.
Values may be sent and summed in bfloat16 or wider, within the bound.
A program may use at most 64 MiB of HBM per device.

v0:
```python
import jax
import jax.numpy as jnp
from jax import lax
from jax.sharding import PartitionSpec as P

KMAX = 128
STEP_SIZE = 0.25
HI = lax.Precision.HIGHEST
NT = (((1,), (1,)), ((), ()))


def window(support_row, start, width):
    below = jnp.sum((support_row < start).astype(jnp.int32))
    local = support_row - start
    inside = (local >= 0) & (local < width)
    slot = jnp.arange(support_row.shape[0]) - below
    chosen = (slot[None, :] == jnp.arange(KMAX)[:, None]) & inside[None, :]
    return jnp.sum(jnp.where(chosen, local[None, :] + 1, 0), axis=1) - 1


def local(matrix, measured, support):
    signals = measured.shape[0]
    n_row = lax.axis_size("row")
    rows_mine = signals // n_row
    columns = matrix.shape[1]
    offset = lax.axis_index("col") * columns
    iterations = support.shape[0]
    total_count = signals * measured.shape[1] * n_row
    lanes = jnp.arange(columns)
    index = [window(support[t], offset, columns) for t in range(iterations)]
    onehot = [(i[:, None] == lanes[None, :]).astype(jnp.bfloat16) for i in index]
    kept = [
        lax.dot_general(e, matrix, NT, preferred_element_type=jnp.float32).astype(jnp.bfloat16)
        for e in onehot[:-1]
    ]
    residual = measured
    current = jnp.zeros((signals, KMAX), jnp.float32)
    energies = []
    for t in range(iterations):
        energies.append(jnp.sum(residual * residual))
        half = residual.astype(jnp.bfloat16)
        if t == iterations - 1:
            break
        part = lax.dot_general(half, kept[t], NT, preferred_element_type=jnp.float32)
        gradient = lax.psum(part.astype(jnp.bfloat16), "row").astype(jnp.float32)
        if t:
            same = (index[t - 1][:, None] == index[t][None, :]) & (index[t] >= 0)[None, :]
            current = jnp.dot(current, same.astype(jnp.float32), precision=HI)
        current = current + STEP_SIZE * gradient
        image = jnp.dot(current.astype(jnp.bfloat16), kept[t], preferred_element_type=jnp.float32)
        residual = measured - lax.psum(image.astype(jnp.bfloat16), "col").astype(jnp.float32)
    gradient = lax.psum_scatter(
        jnp.dot(half, matrix, preferred_element_type=jnp.float32).astype(jnp.bfloat16),
        "row", scatter_dimension=0, tiled=True,
    ).astype(jnp.float32)
    mine = lax.dynamic_slice_in_dim(current, lax.axis_index("row") * rows_mine, rows_mine, 0)
    stepped = jnp.dot(mine, onehot[-2].astype(jnp.float32), precision=HI) + STEP_SIZE * gradient
    keep = jnp.sum(onehot[-1].astype(jnp.float32), axis=0)
    sums = jnp.concatenate([jnp.sum(stepped * stepped, axis=0), jnp.stack(energies)])
    sums = lax.psum(sums, "row")
    return (stepped * keep[None, :], jnp.sqrt(sums[:columns]), sums[columns:] / total_count)


def solution(mesh):
    placed = (P("row", "col"), P(None, "row"), P())
    return jax.shard_map(
        local,
        mesh=mesh,
        in_specs=placed,
        out_specs=(P("row", "col"), P("col"), P()),
        check_vma=False,
    )
```

profile of v0, /device:TPU:0, one launch (start us, length us, event | category | flops | bytes accessed | tf_op | source)
XLA Modules:
  0.0 428.1 jit_solution(17295335813921915850)
XLA Ops:
  8.2 1.6 subtract_add_fusion
  9.8 1.3 iota_subtract_fusion.2
  11.3 3.8 fusion.5
  16.2 3.7 fusion.4
  19.9 19.9 %all-reduce.7.cloned.1.call-done = bf16[256,128]{0,1:T(8,128)(2,1)} async-done(((bf16[256,128]{0,1:T(8,128)(2,1)}), bf16[256,128]{0,1:T(8,128)(2,1)}) %all-reduce.7.cloned.1.call-update) | async-done | bytes 65552 | tf_op jit(solution)/shard_map/psum | solution.py:45
  39.8 1.8 convolution_convert_fusion.3
  41.6 1.3 iota_subtract_fusion
  43.1 90.4 %all-reduce.9.cloned.1.call-done = bf16[256,512]{1,0:T(8,128)(2,1)} async-done(((bf16[256,512]{1,0:T(8,128)(2,1)}), bf16[256,512]{1,0:T(8,128)(2,1)}) %all-reduce.9.cloned.1.call-update) | async-done | bytes 262160 | tf_op jit(solution)/shard_map/psum | solution.py:51
  133.4 1.8 convolution_convert_fusion.5
  135.3 22.4 %all-reduce.11.cloned.1.call-done = bf16[256,128]{0,1:T(8,128)(2,1)} async-done(((bf16[256,128]{0,1:T(8,128)(2,1)}), bf16[256,128]{0,1:T(8,128)(2,1)}) %all-reduce.11.cloned.1.call-update) | async-done | bytes 65552 | tf_op jit(solution)/shard_map/psum | solution.py:45
  157.7 1.2 convolution_add_fusion.2
  158.9 1.0 convolution_convert_fusion.2
  160.0 3.7 fusion.6
  163.7 87.6 %all-reduce.13.cloned.1.call-done = bf16[256,512]{1,0:T(8,128)(2,1)} async-done(((bf16[256,512]{1,0:T(8,128)(2,1)}), bf16[256,512]{1,0:T(8,128)(2,1)}) %all-reduce.13.cloned.1.call-update) | async-done | bytes 262160 | tf_op jit(solution)/shard_map/psum | solution.py:51
  251.3 1.8 convolution_convert_fusion.4
  253.2 22.2 %all-reduce.15.cloned.1.call-done = bf16[256,128]{0,1:T(8,128)(2,1)} async-done(((bf16[256,128]{0,1:T(8,128)(2,1)}), bf16[256,128]{0,1:T(8,128)(2,1)}) %all-reduce.15.cloned.1.call-update) | async-done | bytes 65552 | tf_op jit(solution)/shard_map/psum | solution.py:45
  275.4 1.2 convolution_add_fusion.1
  276.6 1.0 convolution_convert_fusion.1
  277.6 91.3 %all-reduce.17.cloned.1.call-done = bf16[256,512]{1,0:T(8,128)(2,1)} async-done(((bf16[256,512]{1,0:T(8,128)(2,1)}), bf16[256,512]{1,0:T(8,128)(2,1)}) %all-reduce.17.cloned.1.call-update) | async-done | bytes 262160 | tf_op jit(solution)/shard_map/psum | solution.py:51
  368.9 4.9 %convolution_convert_fusion = bf16[256,4096]{1,0:T(8,128)(2,1)} fusion(bf16[512,4096]{1,0:T(8,128)(2,1)} %param.3, f32[256,512]{1,0:T(8,128)S(1)} %copy-done, bf16[256,512]{1,0:T(8,128)(2,1)} %all-reduce.17.cloned.1.call-done), kind=kOutput, calls=%fused_computation | convolution fusion | flops 1075183616 | bytes 7077888 | tf_op jit(solution)/shard_map/dot_general | solution.py:53
  375.8 30.5 %reduce-scatter.2.cloned.1.call-done = bf16[128,4096]{1,0:T(8,128)(2,1)} async-done(((bf16[256,4096]{1,0:T(8,128)(2,1)}), bf16[128,4096]{1,0:T(8,128)(2,1)}) %reduce-scatter.2.cloned.1.call-update) | async-done | bytes 1048592 | tf_op jit(solution)/shard_map/reduce_scatter | solution.py:52
  406.4 4.1 multiply_reduce_fusion
  410.4 2.6 concatenate.3
  413.1 7.1 %psum.55 = f32[4100]{0:T(1024)S(1)} all-reduce(f32[4100]{0:T(1024)S(1)} %concatenate.3), channel_id=1, replica_groups=mesh['row'=2,'col'=16] {'row'}, use_global_device_ids=true, to_apply=%region_21.22 | all-reduce | flops 4100 | bytes 32800 | tf_op jit(solution)/shard_map/psum | solution.py:60
  (38 shorter events, 5.9 us)
Async XLA Ops:
  7.2 32.6 %all-reduce.7.cloned.1.call-start = ((), (), s32[]{:S(2)}) async-start(), calls=%async_computation.1 | async-start | bytes 131072 | tf_op jit(solution)/shard_map/psum | solution.py:45
  11.3 3.8 copy-start
  15.9 117.5 %all-reduce.9.cloned.1.call-start = ((), (), s32[]{:S(2)}) async-start(), calls=%async_computation.2 | async-start | bytes 524288 | tf_op jit(solution)/shard_map/psum | solution.py:51
  41.6 116.1 %all-reduce.11.cloned.1.call-start = ((), (), s32[]{:S(2)}) async-start(), calls=%async_computation.3 | async-start | bytes 131072 | tf_op jit(solution)/shard_map/psum | solution.py:45
  135.3 116.0 %all-reduce.13.cloned.1.call-start = ((), (), s32[]{:S(2)}) async-start(), calls=%async_computation.4 | async-start | bytes 524288 | tf_op jit(solution)/shard_map/psum | solution.py:51
  159.9 115.5 %all-reduce.15.cloned.1.call-start = ((), (), s32[]{:S(2)}) async-start(), calls=%async_computation.5 | async-start | bytes 131072 | tf_op jit(solution)/shard_map/psum | solution.py:45
  253.1 115.8 %all-reduce.17.cloned.1.call-start = ((), (), s32[]{:S(2)}) async-start(), calls=%async_computation.6 | async-start | bytes 524288 | tf_op jit(solution)/shard_map/psum | solution.py:51
  277.5 128.8 %reduce-scatter.2.cloned.1.call-start = ((), (), s32[]{:S(2)}) async-start(), calls=%async_computation.7 | async-start | bytes 3145728 | tf_op jit(solution)/shard_map/reduce_scatter | solution.py:52
  373.8 0.9 copy-start.1
  373.8 1.0 copy-start.2
  373.8 1.1 copy-start.3
Sparse Core Ops, SparseCore 0:
  16.0 23.6 all-reduce.6
  43.7 89.6 all-reduce.8
  136.3 21.4 all-reduce.10
  161.5 89.6 all-reduce.12
  253.9 21.4 all-reduce.14
  279.2 89.6 all-reduce.16
  373.9 32.3 reduce-scatter.1
where the time goes:
time: 429 us; the launch traced here: 428 us
  waiting for transfers between devices  364 us (85%)
  matrix products  30.6 us (7%)
  between operations  14.2 us (3%)
  other arithmetic  7.66 us (2%)
  blocking collectives  7.1 us (2%)
    psum x3, waiting for transfers between devices, local(): lax.psum(image.astype(jnp.bfloat16), 'col').astype(jnp.float32)  269 us
    psum x3, waiting for transfers between devices, local(): gradient = lax.psum(part.astype(jnp.bfloat16), 'row').astype(jnp.float32)  64.5 us
    reduce_scatter x1, waiting for transfers between devices, local(): lax.psum_scatter(jnp.dot(half, matrix, preferred_element_type=jnp.float32...  30.5 us
    dot_general x3, matrix products, local(): lax.dot_general(e, matrix, NT, preferred_element_type=jnp.float32)  11.1 us
  transfers between devices with their start and end apart: 7, of which 7 were waited for; matrix products, arithmetic and copies ran while one was open for 2% of the time, Pallas kernels for 0%

commit v1 on v0

v1 whole, which is shorter than its diff:
```python
import functools

import jax
import jax.numpy as jnp
from jax import lax
from jax.experimental import pallas as pl
from jax.experimental.pallas import tpu as pltpu
from jax.sharding import PartitionSpec as P

MESH = pl.DeviceIdType.MESH
KMAX = 128
STEP_SIZE = 0.25
CHUNK = 512
BF = jnp.bfloat16
F32 = jnp.float32
NT = (((1,), (1,)), ((), ()))


def nn(a, b):
    return jnp.dot(a, b, preferred_element_type=F32)


def nt(a, b):
    return lax.dot_general(a, b, NT, preferred_element_type=F32)


def split(v):
    hi = v.astype(BF)
    return hi, (v - hi.astype(F32)).astype(BF)


def sizes(n_row, n_col, signals, mb, columns, iterations):
    chips = n_col // 2
    mine = signals // n_row // 2
    groups = max(1, min(mine // 16, chips))
    parts = chips // groups
    total = mb * n_row
    return dict(
        n_row=n_row, chips=chips, mine=mine, gs=groups, gm=parts, ps=mine // groups, pm=total // parts,
        mb=mb, columns=columns, iters=iterations, half=signals // n_row, signals=signals,
        gr=parts // n_row, ahead=(columns * 7 // 16) // CHUNK * CHUNK if n_row == 2 else 0,
    )


def kernel(
    s, supp_ref, meas_ref, a_ref, out_ref, sums_ref, en_ref,
    a_vm, meas_vm, mpiece, onehot, kept, part_send, part_recv, img, rs, res, fin, foth,
    cur_send, cur_recv, qsend, qrecv, a_peer, nrm_send, nrm_recv, e_send, e_recv, e_both,
    a_sem, m_sem, mp_sem, send, kept_recv, kept_core, part_sem, rs_sem, ag_sem, fin_sem, foth_sem,
    core_sem, q_sem, ap_sem, nrm_sem, e_sem,
):
    n_row, chips, mine, gs, gm, ps, pm = (s[k] for k in ("n_row", "chips", "mine", "gs", "gm", "ps", "pm"))
    mb, columns, iters, half, gr, ahead = (s[k] for k in ("mb", "columns", "iters", "half", "gr", "ahead"))
    x = lax.axis_index("row")
    col = lax.axis_index("col")
    chip = col // 2
    core = col % 2
    other = 1 - core
    counter = [0]
    sends = []

    def put(src, dst, recv, row, column):
        copy = pltpu.make_async_remote_copy(
            src_ref=src, dst_ref=dst, send_sem=send.at[counter[0]], recv_sem=recv,
            device_id={"row": row, "col": column}, device_id_type=MESH,
        )
        copy.start()
        counter[0] += 1
        sends.append(copy)

    def drain():
        for copy in sends:
            copy.wait_send()
        sends.clear()

    def took(ref, sem):
        pltpu.make_async_copy(ref, ref, sem).wait()

    def row_at(d):
        return lax.rem(x + d, n_row)

    def row_from(d):
        return lax.rem(x + n_row - d, n_row)

    def chip_at(k):
        return lax.rem(chip + k, chips)

    partner = chip * 2 + other

    strips = 4
    strip = mb // strips
    loads = [
        pltpu.make_async_copy(a_ref.at[pl.ds(i * strip, strip)], a_vm.at[pl.ds(i * strip, strip)], a_sem.at[i])
        for i in range(strips)
    ]
    for load in loads:
        load.start()
    meas_load = pltpu.make_async_copy(meas_ref, meas_vm, m_sem)
    meas_load.start()

    barrier = pltpu.get_barrier_semaphore()
    greeted = 0
    for d in range(n_row):
        for k in range(chips):
            if d or k:
                pl.semaphore_signal(
                    barrier, inc=1, device_id={"row": row_at(d), "col": chip_at(k) * 2 + core}, device_id_type=MESH
                )
                greeted += 1
        pl.semaphore_signal(barrier, inc=1, device_id={"row": row_at(d), "col": partner}, device_id_type=MESH)
        greeted += 1

    k_all = supp_ref.shape[1]
    lane_k = lax.broadcasted_iota(jnp.int32, (1, k_all), 1).astype(F32)
    slot_k = lax.broadcasted_iota(jnp.int32, (KMAX, k_all), 0).astype(F32)
    eye = lax.broadcasted_iota(jnp.int32, (KMAX, KMAX), 0) == lax.broadcasted_iota(jnp.int32, (KMAX, KMAX), 1)
    lane_n = lax.broadcasted_iota(jnp.int32, (1, columns), 1).astype(F32)

    def window(t, block):
        row = supp_ref[pl.ds(t, 1), :].astype(F32)
        start = (block * columns).astype(F32)
        below = jnp.sum((row < start).astype(F32), axis=1, keepdims=True)
        inside = (row >= start) & (row < start + columns)
        chosen = ((lane_k - below) == slot_k) & inside
        return jnp.sum(jnp.where(chosen, row + 1.0, 0.0), axis=1, keepdims=True) - 1.0

    def as_row(index):
        return jnp.sum(jnp.where(eye, index, 0.0), axis=0, keepdims=True)

    def marks(t):
        return (window(t, col) - (col * columns).astype(F32)) == lane_n

    def place_onehot(t):
        onehot[t] = jnp.where(marks(t), 1.0, 0.0).astype(BF)

    my_slots = pl.ds(pl.multiple_of(core * KMAX, KMAX), KMAX)

    def gather_kept(t):
        for i in range(strips):
            if t == 0:
                loads[i].wait()
            picked = nt(onehot[t], a_vm[i * strip:(i + 1) * strip, :])
            kept[t, x, my_slots, i * strip:(i + 1) * strip] = picked.astype(BF)

    def send_kept(t):
        mine_kept = kept.at[t, x, my_slots]
        put(mine_kept, mine_kept, kept_core.at[t, 0], x, partner)
        for d in range(1, n_row):
            put(mine_kept, mine_kept, kept_recv.at[t, d - 1], row_at(d), col)

    def relay_kept(t):
        for d in range(1, n_row):
            got = kept.at[t, row_from(d), my_slots]
            took(got, kept_recv.at[t, d - 1])
            put(got, got, kept_core.at[t, d], x, partner)

    def wait_kept(t):
        for d in range(n_row):
            took(kept.at[t, 0, pl.ds(0, KMAX)], kept_core.at[t, d])

    place_onehot(0)
    gather_kept(0)
    pl.semaphore_wait(barrier, greeted)
    send_kept(0)

    meas_load.wait()
    kept_mine = kept[0, x, my_slots, :]
    part = nt(meas_vm[...].astype(BF), kept_mine).astype(BF)
    for r in range(n_row):
        for c in range(2):
            base = r * half + c * mine
            part_send[r, c] = part[base:base + mine]
    for d in range(n_row):
        if d:
            put(part_send.at[row_at(d), core], part_recv.at[2 * d + core], part_sem, row_at(d), col)
        put(part_send.at[row_at(d), other], part_recv.at[2 * d + core], part_sem, row_at(d), partner)
    part_recv[core] = part_send[x, core]

    gi = chip // gm
    gj = lax.rem(chip, gm)
    owner_row = gj // gr
    piece_lane = pl.ds(pl.multiple_of(lax.rem(gj, gr) * pm, 128), pm)

    def piece_rows(r):
        return pl.ds(pl.multiple_of(r * half + core * mine + gi * ps, 8), ps)

    mp_from = counter[0]
    counter[0] += n_row - 1

    def mp_copy(d):
        return pltpu.make_async_remote_copy(
            src_ref=meas_ref.at[piece_rows(row_at(d)), piece_lane], dst_ref=mpiece,
            send_sem=send.at[mp_from + d - 1], recv_sem=mp_sem,
            device_id={"row": row_at(d), "col": col}, device_id_type=MESH,
        )

    @pl.when(owner_row == x)
    def _():
        pltpu.make_async_copy(meas_ref.at[piece_rows(x), piece_lane], mpiece, mp_sem).start()
        for d in range(1, n_row):
            mp_copy(d).start()

    def global_row(t):
        return jnp.concatenate([as_row(window(t, chip * 2)), as_row(window(t, chip * 2 + 1))], axis=1)

    def global_col(t):
        return jnp.concatenate([window(t, chip * 2), window(t, chip * 2 + 1)], axis=0)

    def same_slots(t):
        row = global_row(t)
        return jnp.where((global_col(t - 1) == row) & (row >= 0.0), 1.0, 0.0).astype(BF)

    def energy(v):
        return jnp.sum(v * v, axis=0, keepdims=True)

    def prefetch(i, count):
        width = ahead // count
        for d in range(1, n_row):
            piece = pl.ds(i * width, width)
            put(a_vm.at[:, piece], a_peer.at[d - 1, :, piece], ap_sem, row_at(d), col)

    current = None
    energies = []
    for t in range(iters - 1):
        if t == 0:
            relay_kept(0)
            took(part_recv.at[pl.ds(0, 2 * n_row - 1)], part_sem)
            gradient = jnp.concatenate(
                [sum(part_recv[2 * d + b].astype(F32) for d in range(n_row)) for b in range(2)], axis=1
            )
            current = STEP_SIZE * gradient
            wait_kept(0)
        else:
            rows = [
                jnp.concatenate(
                    [
                        jnp.concatenate([res[t, g * gm + r * gr + j] for j in range(gr)], axis=1)
                        for g in range(gs)
                    ],
                    axis=0,
                )
                for r in range(n_row)
            ]
            gradient = sum(nt(rows[r], kept[t, r]) for r in range(n_row))
            hi, lo = split(current)
            moved = same_slots(t)
            current = nn(hi, moved) + nn(lo, moved) + STEP_SIZE * gradient
        rounded = current.astype(BF)
        for r in range(n_row):
            image = nn(rounded, kept[t, r]).astype(BF)
            for g in range(gs):
                for j in range(gr):
                    img[t, g * gm + r * gr + j] = image[g * ps:(g + 1) * ps, j * pm:(j + 1) * pm]
        for k in range(1, chips):
            put(img.at[t, chip_at(k)], rs.at[t, k - 1], rs_sem.at[t], x, chip_at(k) * 2 + core)
        if t == 0:
            place_onehot(1)
            gather_kept(1)
            send_kept(1)
            took(mpiece, mp_sem)
            energies.append(energy(mpiece[...]))
        took(rs.at[t], rs_sem.at[t])
        summed = img[t, chip].astype(F32) + sum(rs[t, k].astype(F32) for k in range(chips - 1))
        residual = mpiece[...] - summed
        energies.append(energy(residual))
        last = t == iters - 2
        if not last:
            res[t + 1, chip] = residual.astype(BF)
            for k in range(1, chips):
                piece = res.at[t + 1, chip]
                put(piece, piece, ag_sem.at[t], x, chip_at(k) * 2 + core)
            if t == 0:
                relay_kept(1)
                for u in range(2, iters - 1):
                    place_onehot(u)
                    gather_kept(u)
                    send_kept(u)
                if ahead:
                    for i in range(4):
                        prefetch(i, 4)
                wait_kept(1)
            if t == 1:
                for u in range(2, iters - 1):
                    relay_kept(u)
                    wait_kept(u)
            took(res.at[0, pl.ds(0, chips - 1)], ag_sem.at[t])
        else:
            fin[core, chip] = residual.astype(BF)

    last_piece = fin.at[core, chip]
    foth_from = counter[0]
    counter[0] += chips
    away = lax.rem(owner_row + n_row - x, n_row)
    slot = gi * gr + lax.rem(gj, gr)

    def foth_copy(k):
        return pltpu.make_async_remote_copy(
            src_ref=last_piece, dst_ref=foth.at[jnp.maximum(away - 1, 0), core, slot],
            send_sem=send.at[foth_from + k], recv_sem=foth_sem,
            device_id={"row": owner_row, "col": chip_at(k) * 2 + core}, device_id_type=MESH,
        )

    @pl.when(away > 0)
    def _():
        for k in range(chips):
            foth_copy(k).start()

    for k in range(1, chips):
        put(last_piece, last_piece, fin_sem, x, chip_at(k) * 2 + core)

    lanes = e_send.shape[2]
    folded = [sum(e[:, i * lanes:(i + 1) * lanes] for i in range(pm // lanes)) for e in energies]
    for t in range(iters):
        e_send[t] = folded[t]
    for d in range(n_row):
        for k in range(chips):
            if d or k:
                put(e_send, e_recv.at[d * chips + k - 1], e_sem.at[0], row_at(d), chip_at(k) * 2 + core)

    for b in range(2):
        cur_send[b] = current[:, b * KMAX:(b + 1) * KMAX]
    put(cur_send.at[other], cur_recv.at[core], core_sem.at[0], x, partner)
    cur_recv[core] = cur_send[core]

    keep = jnp.sum(jnp.where(marks(iters - 1), 1.0, 0.0), axis=0, keepdims=True)

    took(foth.at[:, 0], foth_sem)
    for d in range(1, n_row):
        got = foth.at[d - 1, core]
        put(got, got, core_sem.at[1 + d], x, partner)
    took(fin.at[0, pl.ds(0, chips - 1)], fin_sem)
    put(fin.at[core], fin.at[core], core_sem.at[1], x, partner)
    for d in range(1, n_row):
        took(foth.at[d - 1, 0], core_sem.at[1 + d])

    count = columns // CHUNK
    first = ahead // CHUNK
    for d in range(1, n_row):
        theirs = jnp.concatenate(
            [
                jnp.concatenate([foth[d - 1, c, g * gr + j] for j in range(gr)], axis=1)
                for c in range(2) for g in range(gs)
            ],
            axis=0,
        )
        for i in range(first, count):
            qsend[d - 1, i - first] = nn(theirs, a_vm[:, i * CHUNK:(i + 1) * CHUNK]).astype(BF)
            put(qsend.at[d - 1, i - first], qrecv.at[d - 1, i - first], q_sem.at[d - 1, i - first], row_from(d), col)

    took(fin.at[0], core_sem.at[1])
    took(cur_recv.at[0], core_sem.at[0])

    def residual_of(r):
        return jnp.concatenate(
            [
                jnp.concatenate([fin[c, g * gm + r * gr + j] for j in range(gr)], axis=1)
                for c in range(2) for g in range(gs)
            ],
            axis=0,
        )

    own = residual_of(x)
    last_hi, last_lo = split(jnp.concatenate([cur_recv[0], cur_recv[1]], axis=0))

    def finish(i, extra):
        at = slice(i * CHUNK, (i + 1) * CHUNK)
        marked = onehot[iters - 2, :, at]
        stepped = nn(last_hi, marked) + nn(last_lo, marked)
        stepped = stepped + STEP_SIZE * (nn(own, a_vm[:, at]) + extra)
        out_ref[:, at] = stepped * keep[:, at]
        nrm_send[i] = jnp.sum(stepped * stepped, axis=0, keepdims=True)

    if ahead:
        took(a_peer, ap_sem)
        peers = [residual_of(row_from(d)) for d in range(1, n_row)]
        for i in range(first):
            at = slice(i * CHUNK, (i + 1) * CHUNK)
            finish(i, sum(nn(peers[d - 1], a_peer[d - 1, :, at]) for d in range(1, n_row)))
        for d in range(1, n_row):
            piece = pl.ds(0, first)
            put(nrm_send.at[piece], nrm_recv.at[d - 1, piece], nrm_sem.at[0], row_at(d), col)

    took(e_recv, e_sem.at[0])
    total = e_send[...] + sum(e_recv[k] for k in range(n_row * chips - 1))
    e_both[0] = total
    put(e_both.at[0], e_both.at[1], e_sem.at[1], x, partner)

    for i in range(first, count):
        for d in range(1, n_row):
            took(qrecv.at[d - 1, i - first], q_sem.at[d - 1, i - first])
        finish(i, sum(qrecv[d - 1, i - first].astype(F32) for d in range(1, n_row)))
    for d in range(1, n_row):
        piece = pl.ds(first, count - first)
        put(nrm_send.at[piece], nrm_recv.at[d - 1, piece], nrm_sem.at[1], row_at(d), col)

    took(e_both.at[1], e_sem.at[1])
    en_ref[...] = e_both[0] + e_both[1]
    if ahead:
        took(nrm_recv.at[:, pl.ds(0, first)], nrm_sem.at[0])
    took(nrm_recv.at[:, pl.ds(first, count - first)], nrm_sem.at[1])
    sums_ref[...] = nrm_send[...] + sum(nrm_recv[d - 1] for d in range(1, n_row))

    drain()

    @pl.when(owner_row == x)
    def _():
        for d in range(1, n_row):
            mp_copy(d).wait_send()

    @pl.when(away > 0)
    def _():
        for k in range(chips):
            foth_copy(k).wait_send()


def local(matrix, measured, support):
    signals, mb = measured.shape
    columns = matrix.shape[1]
    iters = support.shape[0]
    n_row = lax.axis_size("row")
    n_col = lax.axis_size("col")
    s = sizes(n_row, n_col, signals, mb, columns, iters)
    chips, mine, ps, pm, gs, gr, half = (s[k] for k in ("chips", "mine", "ps", "pm", "gs", "gr", "half"))
    count = columns // CHUNK
    late = count - s["ahead"] // CHUNK
    peers = n_row - 1
    dma = pltpu.SemaphoreType.DMA
    vm = pltpu.VMEM
    outs = pl.pallas_call(
        functools.partial(kernel, s),
        out_shape=(
            jax.ShapeDtypeStruct((half, columns), F32),
            jax.ShapeDtypeStruct((count, 1, CHUNK), F32),
            jax.ShapeDtypeStruct((iters, 1, 128), F32),
        ),
        in_specs=[
            pl.BlockSpec(memory_space=vm),
            pl.BlockSpec(memory_space=pltpu.HBM),
            pl.BlockSpec(memory_space=pltpu.HBM),
        ],
        out_specs=(pl.BlockSpec(memory_space=vm),) * 3,
        scratch_shapes=[
            vm((mb, columns), BF),
            vm((signals, mb), F32),
            vm((ps, pm), F32),
            vm((iters - 1, KMAX, columns), BF),
            vm((iters - 1, n_row, 2 * KMAX, mb), BF),
            vm((n_row, 2, mine, KMAX), BF),
            vm((2 * n_row, mine, KMAX), BF),
            vm((iters - 1, chips, ps, pm), BF),
            vm((iters - 1, chips - 1, ps, pm), BF),
            vm((iters - 1, chips, ps, pm), BF),
            vm((2, chips, ps, pm), BF),
            vm((peers, 2, gs * gr, ps, pm), BF),
            vm((2, mine, KMAX), F32),
            vm((2, mine, KMAX), F32),
            vm((peers, late, half, CHUNK), BF),
            vm((peers, late, half, CHUNK), BF),
            vm((peers, mb, max(s["ahead"], 128)), BF),
            vm((count, 1, CHUNK), F32),
            vm((peers, count, 1, CHUNK), F32),
            vm((iters, 1, 128), F32),
            vm((n_row * chips - 1, iters, 1, 128), F32),
            vm((2, iters, 1, 128), F32),
            dma((4,)),
            dma,
            dma,
            dma((512 if n_row == 2 else 1024,)),
            dma((iters - 1, peers)),
            dma((iters - 1, n_row)),
            dma,
            dma((iters - 1,)),
            dma((iters - 1,)),
            dma,
            dma,
            dma((2 + n_row,)),
            dma((peers, late)),
            dma,
            dma((2,)),
            dma((2,)),
        ],
        compiler_params=pltpu.CompilerParams(
            collective_id=0, has_side_effects=True, vmem_limit_bytes=60 * 1024 * 1024
        ),
    )(support, measured, matrix)
    estimate, squares, energy = outs
    entries = signals * mb * n_row
    return (
        estimate,
        jnp.sqrt(squares.reshape(columns)),
        jnp.sum(energy, axis=(1, 2)) / entries,
    )


def solution(mesh):
    placed = (P("row", "col"), P(None, "row"), P())
    return jax.shard_map(
        local,
        mesh=mesh,
        in_specs=placed,
        out_specs=(P("row", "col"), P("col"), P()),
        check_vma=False,
    )
```

time: 429 us -> 94.6 us (0.22)
  waiting for transfers between devices: 364 us -> 0 us
  Pallas kernels: 0 us -> 87.8 us
  matrix products: 30.6 us -> 0 us
  between operations: 14.2 us -> 0.64 us
  blocking collectives: 7.1 us -> 0 us
  other arithmetic: 7.66 us -> 1.3 us
    psum x6 -> x0, waiting for transfers between devices: 334 us -> none  [the longest x3 269 us: local(): lax.psum(image.astype(jnp.bfloat16), 'col').astype(jnp.float32)]
    pallas_call x0 -> x1, Pallas kernels: none -> 87.8 us  [local(): pl.pallas_call(functools.partial(kernel, s), out_shape=(jax.ShapeDtypeStr...]
    dot_general x13 -> x0, matrix products: 30.6 us -> none  [the longest x3 11.1 us: local(): lax.dot_general(e, matrix, NT, preferred_element_type=jnp.float32)]
    reduce_scatter x1 -> x0, waiting for transfers between devices: 30.5 us -> none  [local(): lax.psum_scatter(jnp.dot(half, matrix, preferred_element_type=jnp.float32...]
    psum x1 -> x0, blocking collectives: 7.1 us -> none  [local(): sums = lax.psum(sums, 'row')]
  transfers between devices with their start and end apart: 7 -> 0, of which waited for: 7 -> 0; matrix products, arithmetic and copies ran while one was open for 2% -> 0% of each run, Pallas kernels for 0% -> 0%
where the time goes in v1:
time: 94.6 us; the launch traced here: 94.3 us
  Pallas kernels  87.8 us (93%)
  local copies, waits for them, and re-layouts  4.47 us (5%)
  other arithmetic  1.3 us (1%)
    pallas_call x1, Pallas kernels, local(): pl.pallas_call(functools.partial(kernel, s), out_shape=(jax.ShapeDtypeStr...  87.8 us
    unnamed x1, local copies, waits for them, and re-layouts  3.11 us

profile of v1, /device:TPU:0, one launch (start us, length us, event | category | flops | bytes accessed | tf_op | source)
XLA Modules:
  0.0 94.3 jit_solution(5422539391217913260)
XLA Ops:
  0.6 87.8 %shard_map.58 = (f32[128,4096]{1,0:T(8,128)}, f32[8,1,512]{2,1,0:T(1,128)}, f32[4,1,128]{2,1,0:T(1,128)}) custom-call(s32[4,1024]{1,0:T(4,128)} %supp_ref.1, f32[256,512]{1,0:T(8,128)} %meas_ref.1, bf16[512,4096]{1,0:T(8,128)(2,1)} %a_ref.1), custom_call_target="tpu_custom_call" | custom-call | tf_op jit(solution)/shard_map/pallas_call | solution.py:429
  88.5 0.8 reduce_sum.9
  89.3 0.5 broadcast_multiply_fusion
  89.8 1.4 %sqrt.6 = f32[8,1,512]{2,1,0:T(1,128)} sqrt(f32[8,1,512]{2,1,0:T(1,128)} %get-tuple-element.7) | non-fusion elementwise | bytes 32768 | tf_op jit(solution)/shard_map/sqrt | solution.py:490
  91.1 3.1 %copy.7 = f32[128,4096]{1,0:T(8,128)} copy(f32[128,4096]{1,0:T(8,128)} %get-tuple-element.12) | data formatting | bytes 4194304

commit v2 on v1

--- a/solution.py
+++ b/solution.py
@@ -10,7 +10,8 @@
 MESH = pl.DeviceIdType.MESH
 KMAX = 128
 STEP_SIZE = 0.25
-CHUNK = 512
+CHUNK = 256
+AHEAD = 1280
 BF = jnp.bfloat16
 F32 = jnp.float32
 NT = (((1,), (1,)), ((), ()))
@@ -38,15 +39,16 @@
     return dict(
         n_row=n_row, chips=chips, mine=mine, gs=groups, gm=parts, ps=mine // groups, pm=total // parts,
         mb=mb, columns=columns, iters=iterations, half=signals // n_row, signals=signals,
-        gr=parts // n_row, ahead=(columns * 7 // 16) // CHUNK * CHUNK if n_row == 2 else 0,
+        gr=parts // n_row, ahead=min(AHEAD, columns // 2) if n_row == 2 else 0,
     )
 
 
 def kernel(
     s, supp_ref, meas_ref, a_ref, out_ref, sums_ref, en_ref,
-    a_vm, meas_vm, mpiece, onehot, kept, part_send, part_recv, img, rs, res, fin, foth,
+    a_vm, mpiece, onehot, same, kept, part_send, part_recv, img, rs, res, fin, foth,
     cur_send, cur_recv, qsend, qrecv, a_peer, nrm_send, nrm_recv, e_send, e_recv, e_both,
-    a_sem, m_sem, mp_sem, send, kept_recv, kept_core, part_sem, rs_sem, ag_sem, fin_sem, foth_sem,
+    a_sem, mp_sem, mp_left, kept_left, part_left, rs_left, ag_left, fin_left, foth_left,
+    q_left, ap_left, nrm_left, e_left, kept_recv, kept_core, part_sem, rs_sem, ag_sem, fin_sem, foth_sem,
     core_sem, q_sem, ap_sem, nrm_sem, e_sem,
 ):
     n_row, chips, mine, gs, gm, ps, pm = (s[k] for k in ("n_row", "chips", "mine", "gs", "gm", "ps", "pm"))
@@ -56,25 +58,19 @@
     chip = col // 2
     core = col % 2
     other = 1 - core
-    counter = [0]
-    sends = []
-
-    def put(src, dst, recv, row, column):
-        copy = pltpu.make_async_remote_copy(
-            src_ref=src, dst_ref=dst, send_sem=send.at[counter[0]], recv_sem=recv,
+    sent = []
+
+    def put(src, dst, left, recv, row, column):
+        pltpu.make_async_remote_copy(
+            src_ref=src, dst_ref=dst, send_sem=left, recv_sem=recv,
             device_id={"row": row, "col": column}, device_id_type=MESH,
-        )
-        copy.start()
-        counter[0] += 1
-        sends.append(copy)
-
-    def drain():
-        for copy in sends:
-            copy.wait_send()
-        sends.clear()
+        ).start()
 
     def took(ref, sem):
         pltpu.make_async_copy(ref, ref, sem).wait()
+
+    def left_later(ref, sem):
+        sent.append((ref, sem))
 
     def row_at(d):
         return lax.rem(x + d, n_row)
@@ -95,8 +91,6 @@
     ]
     for load in loads:
         load.start()
-    meas_load = pltpu.make_async_copy(meas_ref, meas_vm, m_sem)
-    meas_load.start()
 
     barrier = pltpu.get_barrier_semaphore()
     greeted = 0
@@ -136,23 +130,28 @@
     my_slots = pl.ds(pl.multiple_of(core * KMAX, KMAX), KMAX)
 
     def gather_kept(t):
+        if t == 0:
+            for load in loads:
+                load.wait()
         for i in range(strips):
-            if t == 0:
-                loads[i].wait()
             picked = nt(onehot[t], a_vm[i * strip:(i + 1) * strip, :])
             kept[t, x, my_slots, i * strip:(i + 1) * strip] = picked.astype(BF)
 
     def send_kept(t):
         mine_kept = kept.at[t, x, my_slots]
-        put(mine_kept, mine_kept, kept_core.at[t, 0], x, partner)
-        for d in range(1, n_row):
-            put(mine_kept, mine_kept, kept_recv.at[t, d - 1], row_at(d), col)
+        put(mine_kept, mine_kept, kept_left.at[t, 0], kept_core.at[t, 0], x, partner)
+        for d in range(1, n_row):
+            put(mine_kept, mine_kept, kept_left.at[t, 1], kept_recv.at[t, d - 1], row_at(d), col)
+        pieces = kept.at[t, pl.ds(0, n_row - 1), pl.ds(0, KMAX)]
+        left_later(kept.at[t, 0, pl.ds(0, KMAX)], kept_left.at[t, 0])
+        left_later(pieces, kept_left.at[t, 1])
+        left_later(pieces, kept_left.at[t, 2])
 
     def relay_kept(t):
         for d in range(1, n_row):
             got = kept.at[t, row_from(d), my_slots]
             took(got, kept_recv.at[t, d - 1])
-            put(got, got, kept_core.at[t, d], x, partner)
+            put(got, got, kept_left.at[t, 2], kept_core.at[t, d], x, partner)
 
     def wait_kept(t):
         for d in range(n_row):
@@ -163,17 +162,17 @@
     pl.semaphore_wait(barrier, greeted)
     send_kept(0)
 
-    meas_load.wait()
     kept_mine = kept[0, x, my_slots, :]
-    part = nt(meas_vm[...].astype(BF), kept_mine).astype(BF)
+    part = nt(meas_ref[...].astype(BF), kept_mine).astype(BF)
     for r in range(n_row):
         for c in range(2):
             base = r * half + c * mine
             part_send[r, c] = part[base:base + mine]
     for d in range(n_row):
         if d:
-            put(part_send.at[row_at(d), core], part_recv.at[2 * d + core], part_sem, row_at(d), col)
-        put(part_send.at[row_at(d), other], part_recv.at[2 * d + core], part_sem, row_at(d), partner)
+            put(part_send.at[row_at(d), core], part_recv.at[2 * d + core], part_left, part_sem, row_at(d), col)
+        put(part_send.at[row_at(d), other], part_recv.at[2 * d + core], part_left, part_sem, row_at(d), partner)
+    left_later(part_recv.at[pl.ds(0, 2 * n_row - 1)], part_left)
     part_recv[core] = part_send[x, core]
 
     gi = chip // gm
@@ -184,21 +183,23 @@
     def piece_rows(r):
         return pl.ds(pl.multiple_of(r * half + core * mine + gi * ps, 8), ps)
 
-    mp_from = counter[0]
-    counter[0] += n_row - 1
-
     def mp_copy(d):
         return pltpu.make_async_remote_copy(
             src_ref=meas_ref.at[piece_rows(row_at(d)), piece_lane], dst_ref=mpiece,
-            send_sem=send.at[mp_from + d - 1], recv_sem=mp_sem,
+            send_sem=mp_left.at[d - 1], recv_sem=mp_sem,
             device_id={"row": row_at(d), "col": col}, device_id_type=MESH,
         )
 
     @pl.when(owner_row == x)
     def _():
-        pltpu.make_async_copy(meas_ref.at[piece_rows(x), piece_lane], mpiece, mp_sem).start()
+        mpiece[...] = meas_ref[piece_rows(x), piece_lane]
         for d in range(1, n_row):
             mp_copy(d).start()
+
+    for t in range(1, iters - 1):
+        place_onehot(t)
+        gather_kept(t)
+        send_kept(t)
 
     def global_row(t):
         return jnp.concatenate([as_row(window(t, chip * 2)), as_row(window(t, chip * 2 + 1))], axis=1)
@@ -213,11 +214,13 @@
     def energy(v):
         return jnp.sum(v * v, axis=0, keepdims=True)
 
-    def prefetch(i, count):
-        width = ahead // count
-        for d in range(1, n_row):
-            piece = pl.ds(i * width, width)
-            put(a_vm.at[:, piece], a_peer.at[d - 1, :, piece], ap_sem, row_at(d), col)
+    count = columns // CHUNK
+    first = ahead // CHUNK
+
+    def prefetch(i):
+        for d in range(1, n_row):
+            piece = pl.ds(i * CHUNK, CHUNK)
+            put(a_vm.at[:, piece], a_peer.at[d - 1, :, piece], ap_left, ap_sem, row_at(d), col)
 
     current = None
     energies = []
@@ -243,7 +246,7 @@
             ]
             gradient = sum(nt(rows[r], kept[t, r]) for r in range(n_row))
             hi, lo = split(current)
-            moved = same_slots(t)
+            moved = same[t]
             current = nn(hi, moved) + nn(lo, moved) + STEP_SIZE * gradient
         rounded = current.astype(BF)
         for r in range(n_row):
@@ -252,13 +255,21 @@
                 for j in range(gr):
                     img[t, g * gm + r * gr + j] = image[g * ps:(g + 1) * ps, j * pm:(j + 1) * pm]
         for k in range(1, chips):
-            put(img.at[t, chip_at(k)], rs.at[t, k - 1], rs_sem.at[t], x, chip_at(k) * 2 + core)
+            put(img.at[t, chip_at(k)], rs.at[t, k - 1], rs_left.at[t], rs_sem.at[t], x, chip_at(k) * 2 + core)
+        left_later(rs.at[t], rs_left.at[t])
         if t == 0:
-            place_onehot(1)
-            gather_kept(1)
-            send_kept(1)
-            took(mpiece, mp_sem)
+            for i in range(first - 1):
+                prefetch(i)
+
+            @pl.when(owner_row != x)
+            def _():
+                took(mpiece, mp_sem)
+
             energies.append(energy(mpiece[...]))
+            for u in range(1, iters - 1):
+                same[u] = same_slots(u)
+            keep = jnp.sum(jnp.where(marks(iters - 1), 1.0, 0.0), axis=0, keepdims=True)
+            relay_kept(1)
         took(rs.at[t], rs_sem.at[t])
         summed = img[t, chip].astype(F32) + sum(rs[t, k].astype(F32) for k in range(chips - 1))
         residual = mpiece[...] - summed
@@ -268,35 +279,24 @@
             res[t + 1, chip] = residual.astype(BF)
             for k in range(1, chips):
                 piece = res.at[t + 1, chip]
-                put(piece, piece, ag_sem.at[t], x, chip_at(k) * 2 + core)
+                put(piece, piece, ag_left.at[t], ag_sem.at[t], x, chip_at(k) * 2 + core)
+            left_later(res.at[0, pl.ds(0, chips - 1)], ag_left.at[t])
             if t == 0:
-                relay_kept(1)
-                for u in range(2, iters - 1):
-                    place_onehot(u)
-                    gather_kept(u)
-                    send_kept(u)
-                if ahead:
-                    for i in range(4):
-                        prefetch(i, 4)
-                wait_kept(1)
-            if t == 1:
                 for u in range(2, iters - 1):
                     relay_kept(u)
-                    wait_kept(u)
+            wait_kept(t + 1)
             took(res.at[0, pl.ds(0, chips - 1)], ag_sem.at[t])
         else:
             fin[core, chip] = residual.astype(BF)
 
     last_piece = fin.at[core, chip]
-    foth_from = counter[0]
-    counter[0] += chips
     away = lax.rem(owner_row + n_row - x, n_row)
     slot = gi * gr + lax.rem(gj, gr)
 
     def foth_copy(k):
         return pltpu.make_async_remote_copy(
             src_ref=last_piece, dst_ref=foth.at[jnp.maximum(away - 1, 0), core, slot],
-            send_sem=send.at[foth_from + k], recv_sem=foth_sem,
+            send_sem=foth_left, recv_sem=foth_sem,
             device_id={"row": owner_row, "col": chip_at(k) * 2 + core}, device_id_type=MESH,
         )
 
@@ -305,8 +305,12 @@
         for k in range(chips):
             foth_copy(k).start()
 
+    if first:
+        prefetch(first - 1)
     for k in range(1, chips):
-        put(last_piece, last_piece, fin_sem, x, chip_at(k) * 2 + core)
+        put(last_piece, last_piece, fin_left.at[0], fin_sem, x, chip_at(k) * 2 + core)
+
+    left_later(fin.at[0, pl.ds(0, chips - 1)], fin_left.at[0])
 
     lanes = e_send.shape[2]
     folded = [sum(e[:, i * lanes:(i + 1) * lanes] for i in range(pm // lanes)) for e in energies]
@@ -315,26 +319,27 @@
     for d in range(n_row):
         for k in range(chips):
             if d or k:
-                put(e_send, e_recv.at[d * chips + k - 1], e_sem.at[0], row_at(d), chip_at(k) * 2 + core)
+                put(e_send, e_recv.at[d * chips + k - 1], e_left.at[0], e_sem.at[0], row_at(d), chip_at(k) * 2 + core)
+
+    left_later(e_recv, e_left.at[0])
 
     for b in range(2):
         cur_send[b] = current[:, b * KMAX:(b + 1) * KMAX]
-    put(cur_send.at[other], cur_recv.at[core], core_sem.at[0], x, partner)
+    put(cur_send.at[other], cur_recv.at[core], fin_left.at[1], core_sem.at[0], x, partner)
+    left_later(cur_recv.at[0], fin_left.at[1])
     cur_recv[core] = cur_send[core]
-
-    keep = jnp.sum(jnp.where(marks(iters - 1), 1.0, 0.0), axis=0, keepdims=True)
 
     took(foth.at[:, 0], foth_sem)
     for d in range(1, n_row):
         got = foth.at[d - 1, core]
-        put(got, got, core_sem.at[1 + d], x, partner)
+        put(got, got, fin_left.at[2], core_sem.at[1 + d], x, partner)
     took(fin.at[0, pl.ds(0, chips - 1)], fin_sem)
-    put(fin.at[core], fin.at[core], core_sem.at[1], x, partner)
+    put(fin.at[core], fin.at[core], fin_left.at[3], core_sem.at[1], x, partner)
+    left_later(foth.at[:, 0], fin_left.at[2])
+    left_later(fin.at[0], fin_left.at[3])
     for d in range(1, n_row):
         took(foth.at[d - 1, 0], core_sem.at[1 + d])
 
-    count = columns // CHUNK
-    first = ahead // CHUNK
     for d in range(1, n_row):
         theirs = jnp.concatenate(
             [
@@ -345,7 +350,12 @@
         )
         for i in range(first, count):
             qsend[d - 1, i - first] = nn(theirs, a_vm[:, i * CHUNK:(i + 1) * CHUNK]).astype(BF)
-            put(qsend.at[d - 1, i - first], qrecv.at[d - 1, i - first], q_sem.at[d - 1, i - first], row_from(d), col)
+            put(
+                qsend.at[d - 1, i - first], qrecv.at[d - 1, i - first], q_left, q_sem.at[d - 1, i - first],
+                row_from(d), col,
+            )
+
+    left_later(qsend, q_left)
 
     took(fin.at[0], core_sem.at[1])
     took(cur_recv.at[0], core_sem.at[0])
@@ -362,13 +372,17 @@
     own = residual_of(x)
     last_hi, last_lo = split(jnp.concatenate([cur_recv[0], cur_recv[1]], axis=0))
 
+    lines = CHUNK // 128
+
     def finish(i, extra):
         at = slice(i * CHUNK, (i + 1) * CHUNK)
         marked = onehot[iters - 2, :, at]
         stepped = nn(last_hi, marked) + nn(last_lo, marked)
         stepped = stepped + STEP_SIZE * (nn(own, a_vm[:, at]) + extra)
         out_ref[:, at] = stepped * keep[:, at]
-        nrm_send[i] = jnp.sum(stepped * stepped, axis=0, keepdims=True)
+        squares = jnp.sum(stepped * stepped, axis=0, keepdims=True)
+        for j in range(lines):
+            nrm_send[i, j:j + 1] = squares[:, j * 128:(j + 1) * 128]
 
     if ahead:
         took(a_peer, ap_sem)
@@ -378,12 +392,16 @@
             finish(i, sum(nn(peers[d - 1], a_peer[d - 1, :, at]) for d in range(1, n_row)))
         for d in range(1, n_row):
             piece = pl.ds(0, first)
-            put(nrm_send.at[piece], nrm_recv.at[d - 1, piece], nrm_sem.at[0], row_at(d), col)
+            put(nrm_send.at[piece], nrm_recv.at[d - 1, piece], nrm_left.at[0], nrm_sem.at[0], row_at(d), col)
+
+        left_later(nrm_recv.at[:, pl.ds(0, first)], nrm_left.at[0])
+        left_later(a_peer, ap_left)
 
     took(e_recv, e_sem.at[0])
     total = e_send[...] + sum(e_recv[k] for k in range(n_row * chips - 1))
     e_both[0] = total
-    put(e_both.at[0], e_both.at[1], e_sem.at[1], x, partner)
+    put(e_both.at[0], e_both.at[1], e_left.at[1], e_sem.at[1], x, partner)
+    left_later(e_both.at[0], e_left.at[1])
 
     for i in range(first, count):
         for d in range(1, n_row):
@@ -391,16 +409,22 @@
         finish(i, sum(qrecv[d - 1, i - first].astype(F32) for d in range(1, n_row)))
     for d in range(1, n_row):
         piece = pl.ds(first, count - first)
-        put(nrm_send.at[piece], nrm_recv.at[d - 1, piece], nrm_sem.at[1], row_at(d), col)
+        put(nrm_send.at[piece], nrm_recv.at[d - 1, piece], nrm_left.at[1], nrm_sem.at[1], row_at(d), col)
+    left_later(nrm_recv.at[:, pl.ds(first, count - first)], nrm_left.at[1])
 
     took(e_both.at[1], e_sem.at[1])
-    en_ref[...] = e_both[0] + e_both[1]
+    entries = s["signals"] * mb * n_row
+    for t in range(iters):
+        en_ref[t] = jnp.sum(e_both[0, t] + e_both[1, t]) / entries
     if ahead:
         took(nrm_recv.at[:, pl.ds(0, first)], nrm_sem.at[0])
     took(nrm_recv.at[:, pl.ds(first, count - first)], nrm_sem.at[1])
-    sums_ref[...] = nrm_send[...] + sum(nrm_recv[d - 1] for d in range(1, n_row))
-
-    drain()
+    for i in range(count):
+        squares = nrm_send[i] + sum(nrm_recv[d - 1, i] for d in range(1, n_row))
+        sums_ref[i * lines:(i + 1) * lines] = jnp.sqrt(squares)
+
+    for ref, sem in sent:
+        took(ref, sem)
 
     @pl.when(owner_row == x)
     def _():
@@ -409,8 +433,7 @@
 
     @pl.when(away > 0)
     def _():
-        for k in range(chips):
-            foth_copy(k).wait_send()
+        took(fin.at[0], foth_left)
 
 
 def local(matrix, measured, support):
@@ -430,20 +453,22 @@
         functools.partial(kernel, s),
         out_shape=(
             jax.ShapeDtypeStruct((half, columns), F32),
-            jax.ShapeDtypeStruct((count, 1, CHUNK), F32),
-            jax.ShapeDtypeStruct((iters, 1, 128), F32),
+            jax.ShapeDtypeStruct((columns // 128, 128), F32),
+            jax.ShapeDtypeStruct((iters,), F32),
         ),
         in_specs=[
             pl.BlockSpec(memory_space=vm),
-            pl.BlockSpec(memory_space=pltpu.HBM),
+            pl.BlockSpec(memory_space=vm),
             pl.BlockSpec(memory_space=pltpu.HBM),
         ],
-        out_specs=(pl.BlockSpec(memory_space=vm),) * 3,
+        out_specs=(
+            pl.BlockSpec(memory_space=vm), pl.BlockSpec(memory_space=vm), pl.BlockSpec(memory_space=pltpu.SMEM)
+        ),
         scratch_shapes=[
             vm((mb, columns), BF),
-            vm((signals, mb), F32),
             vm((ps, pm), F32),
             vm((iters - 1, KMAX, columns), BF),
+            vm((iters - 1, 2 * KMAX, 2 * KMAX), BF),
             vm((iters - 1, n_row, 2 * KMAX, mb), BF),
             vm((n_row, 2, mine, KMAX), BF),
             vm((2 * n_row, mine, KMAX), BF),
@@ -457,15 +482,24 @@
             vm((peers, late, half, CHUNK), BF),
             vm((peers, late, half, CHUNK), BF),
             vm((peers, mb, max(s["ahead"], 128)), BF),
-            vm((count, 1, CHUNK), F32),
-            vm((peers, count, 1, CHUNK), F32),
+            vm((count, CHUNK // 128, 128), F32),
+            vm((peers, count, CHUNK // 128, 128), F32),
             vm((iters, 1, 128), F32),
             vm((n_row * chips - 1, iters, 1, 128), F32),
             vm((2, iters, 1, 128), F32),
             dma((4,)),
             dma,
-            dma,
-            dma((512 if n_row == 2 else 1024,)),
+            dma((peers,)),
+            dma((iters - 1, 3)),
+            dma,
+            dma((iters - 1,)),
+            dma((iters - 1,)),
+            dma((4,)),
+            dma,
+            dma,
+            dma,
+            dma((2,)),
+            dma((2,)),
             dma((iters - 1, peers)),
             dma((iters - 1, n_row)),
             dma,
@@ -480,16 +514,11 @@
             dma((2,)),
         ],
         compiler_params=pltpu.CompilerParams(
-            collective_id=0, has_side_effects=True, vmem_limit_bytes=60 * 1024 * 1024
+            collective_id=0, has_side_effects=True, vmem_limit_bytes=50 * 1024 * 1024
         ),
     )(support, measured, matrix)
-    estimate, squares, energy = outs
-    entries = signals * mb * n_row
-    return (
-        estimate,
-        jnp.sqrt(squares.reshape(columns)),
-        jnp.sum(energy, axis=(1, 2)) / entries,
-    )
+    estimate, norms, energy = outs
+    return estimate, norms.reshape(columns), energy
 
 
 def solution(mesh):

time: 94.6 us -> 71.9 us (0.76)
  Pallas kernels: 87.8 us -> 66.8 us
  other arithmetic: 1.3 us -> 0 us
    pallas_call x1, Pallas kernels: 87.8 us -> 66.8 us  [local(): pl.pallas_call(functools.partial(kernel, s), out_shape=(jax.ShapeDtypeStr...]
    sqrt x1 -> x0, local copies, waits for them, and re-layouts: 1.36 us -> none  [local(): jnp.sqrt(squares.reshape(columns))]
    unnamed x1 -> x7, local copies, waits for them, and re-layouts: 3.11 us -> 4.19 us
where the time goes in v2:
time: 71.9 us; the launch traced here: 71.6 us
  Pallas kernels  66.8 us (93%)
  local copies, waits for them, and re-layouts  4.19 us (6%)
    pallas_call x1, Pallas kernels, local(): pl.pallas_call(functools.partial(kernel, s), out_shape=(jax.ShapeDtypeStr...  66.8 us
    unnamed x7, local copies, waits for them, and re-layouts  4.19 us

profile of v2, /device:TPU:0, one launch (start us, length us, event | category | flops | bytes accessed | tf_op | source)
XLA Modules:
  0.0 71.6 jit_solution(14041460412989433661)
XLA Ops:
  0.6 0.0 copy-start
  0.6 1.0 %copy-done = f32[256,512]{1,0:T(8,128)S(1)} copy-done((f32[256,512]{1,0:T(8,128)S(1)}, f32[256,512]{1,0:T(8,128)}, u32[]{:S(2)}) %copy-start) | copy-done | bytes 524312
  1.7 0.0 copy-start.1
  1.7 0.7 copy-done.1
  2.4 66.8 %shard_map.58 = (f32[128,4096]{1,0:T(8,128)S(1)}, f32[32,128]{1,0:T(8,128)S(1)}, f32[4]{0:T(128)S(1)}) custom-call(s32[4,1024]{1,0:T(4,128)S(1)} %copy-done.1, f32[256,512]{1,0:T(8,128)S(1)} %copy-done, bf16[512,4096]{1,0:T(8,128)(2,1)} %a_ref.1), custom_call_target="tpu_custom_call" | custom-call | tf_op jit(solution)/shard_map/pallas_call | solution.py:452
  69.2 1.3 %copy.9 = f32[128,4096]{1,0:T(8,128)} copy(f32[128,4096]{1,0:T(8,128)S(1)} %get-tuple-element.12) | data formatting | bytes 4194304
  70.5 0.6 copy.10
  71.1 0.5 copy.11
Async XLA Ops:
  0.6 1.0 %copy-start = (f32[256,512]{1,0:T(8,128)S(1)}, f32[256,512]{1,0:T(8,128)}, u32[]{:S(2)}) copy-start(f32[256,512]{1,0:T(8,128)} %meas_ref.1) | copy-start | bytes 1572868
  1.7 0.7 %copy-start.1 = (s32[4,1024]{1,0:T(4,128)S(1)}, s32[4,1024]{1,0:T(4,128)}, u32[]{:S(2)}) copy-start(s32[4,1024]{1,0:T(4,128)} %supp_ref.1) | copy-start | bytes 49156

commit v3 on v2

v3 whole, which is shorter than its diff:
```python
import functools

import jax
import jax.numpy as jnp
from jax import lax
from jax.experimental import pallas as pl
from jax.experimental.pallas import tpu as pltpu
from jax.sharding import PartitionSpec as P

MESH = pl.DeviceIdType.MESH
KMAX = 128
STEP_SIZE = 0.25
CHUNK = 256
AHEAD = 896
LATE = 1
BF = jnp.bfloat16
F32 = jnp.float32
NT = (((1,), (1,)), ((), ()))


def nn(a, b):
    return jnp.dot(a, b, preferred_element_type=F32)


def nt(a, b):
    return lax.dot_general(a, b, NT, preferred_element_type=F32)


def split(v):
    hi = v.astype(BF)
    return hi, (v - hi.astype(F32)).astype(BF)


def sizes(n_row, n_col, signals, mb, columns, iterations):
    chips = n_col // 2
    mine = signals // n_row // 2
    chains = 2 if mine % 32 == 0 else 1
    sub = mine // chains
    groups = max(1, min(sub // 16, chips))
    parts = chips // groups
    total = mb * n_row
    return dict(
        n_row=n_row, chips=chips, mine=mine, chains=chains, sub=sub, gs=groups, gm=parts,
        ps=sub // groups, pm=total // parts, mb=mb, columns=columns, iters=iterations,
        half=signals // n_row, signals=signals, gr=parts // n_row,
        ahead=min(AHEAD, columns // 2) if n_row == 2 else 0,
    )


def cut(start, stop):
    edges = list(range(start, stop, CHUNK)) + [stop]
    if edges[-1] - edges[-2] > 128:
        edges.insert(-1, edges[-1] - 128)
    return [slice(a, b) for a, b in zip(edges[:-1], edges[1:])]


def kernel(
    s, supp_hbm, meas_hbm, a_ref, out_ref, sums_ref,
    a_vm, supp_ref, meas_ref, mpiece, onehot, same, kept, part_send, part_recv, img, rs, first_out, res, fin, foth,
    cur_send, cur_recv, qsend, qrecv, a_peer, nrm_send, nrm_recv, e_send, e_recv, e_both,
    in_sem, a_sem, mp_sem, mp_left, kept_left, part_left, rs_left, ag_left, first_left, fin_left, fin_core_left,
    foth_left, foth_core_left, cur_left, q_left, ap_left, nrm_left, e_left,
    kept_recv, kept_core, part_sem, rs_sem, ag_sem, fin_sem, fin_core, foth_sem, foth_core,
    cur_sem, q_sem, ap_sem, nrm_sem, e_sem,
):
    n_row, chips, mine, gs, gm, ps, pm = (s[k] for k in ("n_row", "chips", "mine", "gs", "gm", "ps", "pm"))
    chains, sub = s["chains"], s["sub"]
    mb, columns, iters, half, gr, ahead = (s[k] for k in ("mb", "columns", "iters", "half", "gr", "ahead"))
    x = lax.axis_index("row")
    col = lax.axis_index("col")
    chip = col // 2
    core = col % 2
    other = 1 - core
    sent = []

    def put(src, dst, left, recv, row, column):
        pltpu.make_async_remote_copy(
            src_ref=src, dst_ref=dst, send_sem=left, recv_sem=recv,
            device_id={"row": row, "col": column}, device_id_type=MESH,
        ).start()

    def took(ref, sem):
        pltpu.make_async_copy(ref, ref, sem).wait()

    def left_later(ref, sem):
        sent.append((ref, sem))

    def row_at(d):
        return lax.rem(x + d, n_row)

    def row_from(d):
        return lax.rem(x + n_row - d, n_row)

    def chip_at(k):
        return lax.rem(chip + k, chips)

    partner = chip * 2 + other

    supp_load = pltpu.make_async_copy(supp_hbm, supp_ref, in_sem.at[0])
    supp_load.start()
    strips = 4
    strip = mb // strips
    loads = [
        pltpu.make_async_copy(a_ref.at[pl.ds(i * strip, strip)], a_vm.at[pl.ds(i * strip, strip)], a_sem.at[i])
        for i in range(strips)
    ]
    for load in loads:
        load.start()

    meas_load = pltpu.make_async_copy(meas_hbm, meas_ref, in_sem.at[1])
    meas_load.start()

    barrier = pltpu.get_barrier_semaphore()
    greeted = 0
    for d in range(n_row):
        for k in range(chips):
            if d or k:
                pl.semaphore_signal(
                    barrier, inc=1, device_id={"row": row_at(d), "col": chip_at(k) * 2 + core}, device_id_type=MESH
                )
                greeted += 1
        pl.semaphore_signal(barrier, inc=1, device_id={"row": row_at(d), "col": partner}, device_id_type=MESH)
        greeted += 1

    k_all = supp_ref.shape[1]
    lane_k = lax.broadcasted_iota(jnp.int32, (1, k_all), 1).astype(F32)
    slot_k = lax.broadcasted_iota(jnp.int32, (KMAX, k_all), 0).astype(F32)
    eye = lax.broadcasted_iota(jnp.int32, (KMAX, KMAX), 0) == lax.broadcasted_iota(jnp.int32, (KMAX, KMAX), 1)
    lane_n = lax.broadcasted_iota(jnp.int32, (1, columns), 1).astype(F32)

    def window(t, block):
        row = supp_ref[pl.ds(t, 1), :].astype(F32)
        start = (block * columns).astype(F32)
        below = jnp.sum((row < start).astype(F32), axis=1, keepdims=True)
        inside = (row >= start) & (row < start + columns)
        chosen = ((lane_k - below) == slot_k) & inside
        return jnp.sum(jnp.where(chosen, row + 1.0, 0.0), axis=1, keepdims=True) - 1.0

    def as_row(index):
        return jnp.sum(jnp.where(eye, index, 0.0), axis=0, keepdims=True)

    def marks(t):
        return (window(t, col) - (col * columns).astype(F32)) == lane_n

    def place_onehot(t):
        onehot[t] = jnp.where(marks(t), 1.0, 0.0).astype(BF)

    my_slots = pl.ds(pl.multiple_of(core * KMAX, KMAX), KMAX)

    def gather_kept(t):
        if t == 0:
            for load in loads:
                load.wait()
        for i in range(0, mb, 128):
            picked = nt(onehot[t], a_vm[i:i + 128, :])
            kept[t, x, my_slots, i:i + 128] = picked.astype(BF)

    def send_kept(t):
        mine_kept = kept.at[t, x, my_slots]
        put(mine_kept, mine_kept, kept_left.at[t, 0], kept_core.at[t, 0], x, partner)
        left_later(kept.at[t, 0, pl.ds(0, KMAX)], kept_left.at[t, 0])
        if t:
            for d in range(1, n_row):
                put(mine_kept, mine_kept, kept_left.at[t, 1], kept_recv.at[t, d - 1], row_at(d), col)
            pieces = kept.at[t, pl.ds(0, n_row - 1), pl.ds(0, KMAX)]
            left_later(pieces, kept_left.at[t, 1])
            left_later(pieces, kept_left.at[t, 2])

    def relay_kept(t):
        for d in range(1, n_row):
            got = kept.at[t, row_from(d), my_slots]
            took(got, kept_recv.at[t, d - 1])
            put(got, got, kept_left.at[t, 2], kept_core.at[t, d], x, partner)

    def wait_kept(t):
        for d in range(n_row if t else 1):
            took(kept.at[t, 0, pl.ds(0, KMAX)], kept_core.at[t, d])

    supp_load.wait()
    place_onehot(0)
    gather_kept(0)
    pl.semaphore_wait(barrier, greeted)
    send_kept(0)

    meas_load.wait()
    kept_mine = kept[0, x, my_slots, :]
    part = nt(meas_ref[...].astype(BF), kept_mine).astype(BF)
    for r in range(n_row):
        for c in range(2):
            base = r * half + c * mine
            part_send[c, r] = part[base:base + mine]
    for d in range(n_row):
        if d:
            put(part_send.at[core], part_recv.at[2 * d + core], part_left, part_sem, row_at(d), col)
        put(part_send.at[other], part_recv.at[2 * d + core], part_left, part_sem, row_at(d), partner)
    left_later(part_recv.at[pl.ds(0, 2 * n_row - 1)], part_left)
    part_recv[core] = part_send[core]

    gi = chip // gm
    gj = lax.rem(chip, gm)
    owner_row = gj // gr
    piece_lane = pl.ds(pl.multiple_of(lax.rem(gj, gr) * pm, 128), pm)

    def piece_rows(r, h):
        return pl.ds(pl.multiple_of(r * half + core * mine + h * sub + gi * ps, 8), ps)

    def mp_copy(d, h):
        return pltpu.make_async_remote_copy(
            src_ref=meas_ref.at[piece_rows(row_at(d), h), piece_lane], dst_ref=mpiece.at[h],
            send_sem=mp_left.at[d - 1, h], recv_sem=mp_sem.at[h],
            device_id={"row": row_at(d), "col": col}, device_id_type=MESH,
        )

    @pl.when(owner_row == x)
    def _():
        for h in range(chains):
            mpiece[h] = meas_ref[piece_rows(x, h), piece_lane]
            for d in range(1, n_row):
                mp_copy(d, h).start()

    place_onehot(1)
    gather_kept(1)
    send_kept(1)

    def global_row(t):
        return jnp.concatenate([as_row(window(t, chip * 2)), as_row(window(t, chip * 2 + 1))], axis=1)

    def global_col(t):
        return jnp.concatenate([window(t, chip * 2), window(t, chip * 2 + 1)], axis=0)

    def same_slots(t):
        row = global_row(t)
        return jnp.where((global_col(t - 1) == row) & (row >= 0.0), 1.0, 0.0).astype(BF)

    def energy(v):
        return jnp.sum(v * v, axis=0, keepdims=True)

    lines = columns // 128
    near = ahead // 128
    early = max(near - LATE, 0)

    def prefetch(i):
        for d in range(1, n_row):
            piece = pl.ds(i * 128, 128)
            put(a_vm.at[:, piece], a_peer.at[d - 1, :, piece], ap_left, ap_sem, row_at(d), col)

    turn = chip // n_row
    to_row = lax.rem(chip + core, n_row)
    first_group = turn // gr
    first_part = lax.rem(turn, gr)
    first_slot = first_group * gm + x * gr + first_part
    first_lane = pl.ds(pl.multiple_of(first_part * pm, 128), pm)

    def first_copy(h):
        return pltpu.make_async_remote_copy(
            src_ref=first_out.at[h], dst_ref=res.at[1, h, first_slot],
            send_sem=first_left.at[h], recv_sem=ag_sem.at[0, h],
            device_id={"row": to_row, "col": col}, device_id_type=MESH,
        )

    def sum_of(t, h):
        took(rs.at[t, h], rs_sem.at[t, h])
        return img[t, h, chip].astype(F32) + sum(rs[t, h, k].astype(F32) for k in range(chips - 1))

    def scatter(t, h):
        for k in range(1, chips):
            put(
                img.at[t, h, chip_at(k)], rs.at[t, h, k - 1], rs_left.at[t, h], rs_sem.at[t, h],
                x, chip_at(k) * 2 + core,
            )
        left_later(rs.at[t, h], rs_left.at[t, h])

    def joined(buffer, r, blocks):
        return jnp.concatenate(
            [
                jnp.concatenate([buffer[b + (g * gm + r * gr + j,)] for j in range(gr)], axis=1)
                for b in blocks for g in range(gs)
            ],
            axis=0,
        )

    took(part_recv.at[pl.ds(0, 2 * n_row - 1)], part_sem)

    def first_step(rows):
        return STEP_SIZE * jnp.concatenate(
            [sum(part_recv[(2 * d + b,) + rows].astype(F32) for d in range(n_row)) for b in range(2)], axis=-1
        )

    wait_kept(0)
    for h in range(chains):
        at = slice(h * sub, (h + 1) * sub)
        rounded = jnp.concatenate([first_step((r, at)) for r in range(n_row)], axis=0).astype(BF)
        image = nn(rounded, kept[0, x]).astype(BF)
        for r in range(n_row):
            for g in range(gs):
                for j in range(gr):
                    place = (g * gr + j) * n_row + lax.rem(r + n_row - lax.rem(core, n_row), n_row)
                    img[0, h, place] = image[
                        r * sub + g * ps:r * sub + (g + 1) * ps, j * pm:(j + 1) * pm
                    ]
        scatter(0, h)
    for t in range(2, iters - 1):
        place_onehot(t)
        gather_kept(t)
        send_kept(t)
    mine_step = first_step((x,))
    current = [mine_step[h * sub:(h + 1) * sub] for h in range(chains)]

    @pl.when(owner_row != x)
    def _():
        for h in range(chains):
            took(mpiece.at[h], mp_sem.at[h])

    energies = [[energy(mpiece[h]) for h in range(chains)]]
    for u in range(1, iters - 1):
        same[u] = same_slots(u)
    keep = jnp.sum(jnp.where(marks(iters - 1), 1.0, 0.0), axis=0, keepdims=True)

    found = []
    for h in range(chains):
        rows = pl.ds(pl.multiple_of(to_row * half + core * mine + h * sub + first_group * ps, 8), ps)
        residual = meas_ref[rows, first_lane] - sum_of(0, h)
        found.append(energy(residual))
        first_out[h] = residual.astype(BF)
        for k in range(1, chips):
            put(
                first_out.at[h], res.at[1, h, first_slot], ag_left.at[0, h], ag_sem.at[0, h],
                to_row, chip_at(k) * 2 + core,
            )
        left_later(rs.at[0, 0], ag_left.at[0, h])

        @pl.when(to_row == x)
        def _():
            res[1, h, first_slot] = first_out[h]

        @pl.when(to_row != x)
        def _():
            first_copy(h).start()

    energies.append(found)
    relay_kept(1)
    for i in range(early):
        prefetch(i)
    wait_kept(1)

    away = lax.rem(owner_row + n_row - x, n_row)
    slot = gi * gr + lax.rem(gj, gr)

    def foth_copy(h, k):
        return pltpu.make_async_remote_copy(
            src_ref=fin.at[core, h, chip], dst_ref=foth.at[jnp.maximum(away - 1, 0), core, h, slot],
            send_sem=foth_left.at[h], recv_sem=foth_sem.at[h],
            device_id={"row": owner_row, "col": chip_at(k) * 2 + core}, device_id_type=MESH,
        )

    for t in range(1, iters - 1):
        carried = []
        for h in range(chains):
            hi, lo = split(current[h])
            carried.append(nn(hi, same[t]) + nn(lo, same[t]))
        for h in range(chains):
            if t == 1:

                @pl.when(to_row == x)
                def _():
                    took(res.at[1, h, pl.ds(0, chips - 1)], ag_sem.at[0, h])

                @pl.when(to_row != x)
                def _():
                    took(res.at[1, h], ag_sem.at[0, h])

            else:
                took(res.at[1, h, pl.ds(0, chips - 1)], ag_sem.at[t - 1, h])
            gradient = sum(nt(joined(res, r, [(t, h)]), kept[t, r]) for r in range(n_row))
            current[h] = carried[h] + STEP_SIZE * gradient
            rounded = current[h].astype(BF)
            for r in range(n_row):
                image = nn(rounded, kept[t, r]).astype(BF)
                for g in range(gs):
                    for j in range(gr):
                        img[t, h, g * gm + r * gr + j] = image[g * ps:(g + 1) * ps, j * pm:(j + 1) * pm]
            scatter(t, h)
        if t + 1 < iters - 1:
            relay_kept(t + 1)
            wait_kept(t + 1)
        found = []
        for h in range(chains):
            residual = mpiece[h] - sum_of(t, h)
            found.append(energy(residual))
            if t < iters - 2:
                res[t + 1, h, chip] = residual.astype(BF)
                piece = res.at[t + 1, h, chip]
                for k in range(1, chips):
                    put(piece, piece, ag_left.at[t, h], ag_sem.at[t, h], x, chip_at(k) * 2 + core)
                left_later(rs.at[0, 0], ag_left.at[t, h])
                continue
            fin[core, h, chip] = residual.astype(BF)

            @pl.when(away > 0)
            def _():
                for k in range(chips):
                    foth_copy(h, k).start()

            if h == chains - 1:
                for i in range(early, near):
                    prefetch(i)
            piece = fin.at[core, h, chip]
            for k in range(1, chips):
                put(piece, piece, fin_left.at[h], fin_sem.at[h], x, chip_at(k) * 2 + core)
            left_later(rs.at[0, 0], fin_left.at[h])
        energies.append(found)

    lanes = e_send.shape[2]
    folded = [
        sum(e[:, i * lanes:(i + 1) * lanes] for e in found for i in range(pm // lanes)) for found in energies
    ]
    for t in range(iters):
        e_send[t] = folded[t]
    for d in range(n_row):
        for k in range(chips):
            if d or k:
                put(e_send, e_recv.at[d * chips + k - 1], e_left.at[0], e_sem.at[0], row_at(d), chip_at(k) * 2 + core)

    left_later(e_recv, e_left.at[0])

    for b in range(2):
        for h in range(chains):
            cur_send[b, h * sub:(h + 1) * sub] = current[h][:, b * KMAX:(b + 1) * KMAX]
    put(cur_send.at[other], cur_recv.at[core], cur_left, cur_sem, x, partner)
    left_later(cur_recv.at[0], cur_left)
    cur_recv[core] = cur_send[core]

    spans = cut(ahead, columns)
    blocks = [(c, h) for c in range(2) for h in range(chains)]

    def relay_foth():
        for h in range(chains):
            took(foth.at[:, 0, h], foth_sem.at[h])
            for d in range(1, n_row):
                got = foth.at[d - 1, core, h]
                put(got, got, foth_core_left.at[h], foth_core.at[h, d - 1], x, partner)

    def wait_foth():
        for h in range(chains):
            for d in range(1, n_row):
                took(foth.at[d - 1, 0, h], foth_core.at[h, d - 1])

    def relay_fin():
        for h in range(chains):
            took(fin.at[0, h, pl.ds(0, chips - 1)], fin_sem.at[h])
            put(fin.at[core, h], fin.at[core, h], fin_core_left.at[h], fin_core.at[h], x, partner)

    def send_sums(c):
        for d in range(1, n_row):
            theirs = jnp.concatenate(
                [
                    jnp.concatenate([foth[d - 1, c, h, g * gr + j] for j in range(gr)], axis=1)
                    for h in range(chains) for g in range(gs)
                ],
                axis=0,
            )
            for i, at in enumerate(spans):
                there = slice(at.start - ahead, at.stop - ahead)
                qsend[d - 1, c, :, there] = nn(theirs, a_vm[:, at]).astype(BF)
                put(
                    qsend.at[d - 1, c, :, there], qrecv.at[d - 1, c, :, there], q_left, q_sem.at[d - 1, c, i],
                    row_from(d), col,
                )

    for h in range(chains):
        left_later(foth.at[:, 0, h], foth_core_left.at[h])
        left_later(fin.at[0, h], fin_core_left.at[h])

    @pl.when(core == 1)
    def _():
        relay_foth()

    @pl.when(core == 0)
    def _():
        wait_foth()

    send_sums(1)

    @pl.when(core == 1)
    def _():
        relay_fin()
        wait_foth()

    @pl.when(core == 0)
    def _():
        relay_foth()
        relay_fin()

    send_sums(0)
    left_later(qsend, q_left)

    for h in range(chains):
        took(fin.at[0, h], fin_core.at[h])
    took(cur_recv.at[0], cur_sem)

    own = joined(fin, x, blocks)
    last_hi, last_lo = split(jnp.concatenate([cur_recv[0], cur_recv[1]], axis=0))

    def finish(at, extra):
        marked = onehot[iters - 2, :, at]
        stepped = nn(last_hi, marked) + nn(last_lo, marked)
        stepped = stepped + STEP_SIZE * (nn(own, a_vm[:, at]) + extra)
        out_ref[:, at] = stepped * keep[:, at]
        squares = jnp.sum(stepped * stepped, axis=0, keepdims=True)
        for j in range(at.start // 128, at.stop // 128):
            nrm_send[j] = squares[:, j * 128 - at.start:(j + 1) * 128 - at.start]

    if ahead:
        took(a_peer, ap_sem)
        peers = [joined(fin, row_from(d), blocks) for d in range(1, n_row)]
        for at in cut(0, ahead):
            finish(at, sum(nn(peers[d - 1], a_peer[d - 1, :, at]) for d in range(1, n_row)))
        for d in range(1, n_row):
            piece = pl.ds(0, near)
            put(nrm_send.at[piece], nrm_recv.at[d - 1, piece], nrm_left.at[0], nrm_sem.at[0], row_at(d), col)
        left_later(nrm_recv.at[:, pl.ds(0, near)], nrm_left.at[0])
        left_later(a_peer, ap_left)

    took(e_recv, e_sem.at[0])
    total = e_send[...] + sum(e_recv[k] for k in range(n_row * chips - 1))
    e_both[0] = total
    put(e_both.at[0], e_both.at[1], e_left.at[1], e_sem.at[1], x, partner)
    left_later(e_both.at[0], e_left.at[1])

    for i, at in enumerate(spans):
        there = slice(at.start - ahead, at.stop - ahead)
        for d in range(1, n_row):
            for c in (1, 0):
                took(qrecv.at[d - 1, c, :, there], q_sem.at[d - 1, c, i])
        finish(at, sum(
            jnp.concatenate([qrecv[d - 1, c, :, there] for c in range(2)], axis=0).astype(F32)
            for d in range(1, n_row)
        ))
    for d in range(1, n_row):
        piece = pl.ds(near, lines - near)
        put(nrm_send.at[piece], nrm_recv.at[d - 1, piece], nrm_left.at[1], nrm_sem.at[1], row_at(d), col)
    left_later(nrm_recv.at[:, pl.ds(near, lines - near)], nrm_left.at[1])

    took(e_both.at[1], e_sem.at[1])
    for t in range(iters):
        sums_ref[columns // 128 + t:columns // 128 + t + 1] = e_both[0, t] + e_both[1, t]
    if ahead:
        took(nrm_recv.at[:, pl.ds(0, near)], nrm_sem.at[0])
    took(nrm_recv.at[:, pl.ds(near, lines - near)], nrm_sem.at[1])
    for i in range(lines):
        squares = nrm_send[i] + sum(nrm_recv[d - 1, i] for d in range(1, n_row))
        sums_ref[i:i + 1] = jnp.sqrt(squares)

    for ref, sem in sent:
        took(ref, sem)

    @pl.when(owner_row == x)
    def _():
        for h in range(chains):
            for d in range(1, n_row):
                mp_copy(d, h).wait_send()

    @pl.when(to_row != x)
    def _():
        for h in range(chains):
            first_copy(h).wait_send()

    @pl.when(away > 0)
    def _():
        for h in range(chains):
            took(fin.at[0, h], foth_left.at[h])


def deliver(entries, est_ref, sums_ref, est_out, norm_out, energy_out, sem):
    parts = 4
    rows = est_ref.shape[0] // parts
    lines = norm_out.shape[0]
    copies = [pltpu.make_async_copy(sums_ref.at[pl.ds(0, lines)], norm_out, sem.at[parts])] + [
        pltpu.make_async_copy(
            est_ref.at[pl.ds(i * rows, rows)], est_out.at[pl.ds(i * rows, rows)], sem.at[i]
        )
        for i in range(parts)
    ]
    for copy in copies:
        copy.start()
    for t in range(energy_out.shape[0]):
        energy_out[t] = jnp.sum(sums_ref[lines + t:lines + t + 1]) / entries
    for copy in copies:
        copy.wait()


def local(matrix, measured, support):
    signals, mb = measured.shape
    columns = matrix.shape[1]
    iters = support.shape[0]
    n_row = lax.axis_size("row")
    n_col = lax.axis_size("col")
    s = sizes(n_row, n_col, signals, mb, columns, iters)
    chips, mine, ps, pm, gs, gr, half = (s[k] for k in ("chips", "mine", "ps", "pm", "gs", "gr", "half"))
    chains = s["chains"]
    late = len(cut(s["ahead"], columns))
    rest = columns - s["ahead"]
    lines = columns // 128
    peers = n_row - 1
    dma = pltpu.SemaphoreType.DMA
    vm = pltpu.VMEM
    outs = pl.pallas_call(
        functools.partial(kernel, s),
        out_shape=(
            pltpu.VMEM((half, columns), F32),
            pltpu.VMEM((columns // 128 + (iters + 7) // 8 * 8, 128), F32),
        ),
        in_specs=[
            pl.BlockSpec(memory_space=pltpu.HBM),
            pl.BlockSpec(memory_space=pltpu.HBM),
            pl.BlockSpec(memory_space=pltpu.HBM),
        ],
        out_specs=(pl.BlockSpec(memory_space=vm), pl.BlockSpec(memory_space=vm)),
        scratch_shapes=[
            vm((mb, columns), BF),
            vm(support.shape, support.dtype),
            vm(measured.shape, F32),
            vm((chains, ps, pm), F32),
            vm((iters - 1, KMAX, columns), BF),
            vm((iters - 1, 2 * KMAX, 2 * KMAX), BF),
            vm((iters - 1, n_row, 2 * KMAX, mb), BF),
            vm((2, n_row, mine, KMAX), BF),
            vm((2 * n_row, n_row, mine, KMAX), BF),
            vm((iters - 1, chains, chips, ps, pm), BF),
            vm((iters - 1, chains, chips - 1, ps, pm), BF),
            vm((chains, ps, pm), BF),
            vm((iters - 1, chains, chips, ps, pm), BF),
            vm((2, chains, chips, ps, pm), BF),
            vm((peers, 2, chains, gs * gr, ps, pm), BF),
            vm((2, mine, KMAX), F32),
            vm((2, mine, KMAX), F32),
            vm((peers, 2, mine, rest), BF),
            vm((peers, 2, mine, rest), BF),
            vm((peers, mb, max(s["ahead"], 128)), BF),
            vm((lines, 1, 128), F32),
            vm((peers, lines, 1, 128), F32),
            vm((iters, 1, 128), F32),
            vm((n_row * chips - 1, iters, 1, 128), F32),
            vm((2, iters, 1, 128), F32),
            dma((2,)),
            dma((4,)),
            dma((chains,)),
            dma((peers, chains)),
            dma((iters - 1, 3)),
            dma,
            dma((iters - 1, chains)),
            dma((iters - 1, chains)),
            dma((chains,)),
            dma((chains,)),
            dma((chains,)),
            dma((chains,)),
            dma((chains,)),
            dma,
            dma,
            dma,
            dma((2,)),
            dma((2,)),
            dma((iters - 1, peers)),
            dma((iters - 1, n_row)),
            dma,
            dma((iters - 1, chains)),
            dma((iters - 1, chains)),
            dma((chains,)),
            dma((chains,)),
            dma((chains,)),
            dma((chains, peers)),
            dma,
            dma((peers, 2, late)),
            dma,
            dma((2,)),
            dma((2,)),
        ],
        compiler_params=pltpu.CompilerParams(
            collective_id=0, has_side_effects=True, vmem_limit_bytes=60 * 1024 * 1024
        ),
    )(support, measured, matrix)
    estimate, norms, energy = pl.pallas_call(
        functools.partial(deliver, signals * mb * n_row),
        out_shape=(
            jax.ShapeDtypeStruct((half, columns), F32),
            jax.ShapeDtypeStruct((columns // 128, 128), F32),
            jax.ShapeDtypeStruct((iters,), F32),
        ),
        in_specs=[pl.BlockSpec(memory_space=vm), pl.BlockSpec(memory_space=vm)],
        out_specs=(
            pl.BlockSpec(memory_space=pltpu.HBM), pl.BlockSpec(memory_space=pltpu.HBM),
            pl.BlockSpec(memory_space=pltpu.SMEM),
        ),
        scratch_shapes=[dma((5,))],
        compiler_params=pltpu.CompilerParams(vmem_limit_bytes=8 * 1024 * 1024),
    )(*outs)
    return estimate, norms.reshape(columns), energy


def solution(mesh):
    placed = (P("row", "col"), P(None, "row"), P())
    return jax.shard_map(
        local,
        mesh=mesh,
        in_specs=placed,
        out_specs=(P("row", "col"), P("col"), P()),
        check_vma=False,
    )
```

time: 71.9 us -> 64.2 us (0.89)
  local copies, waits for them, and re-layouts: 4.19 us -> 0 us
  Pallas kernels: 66.8 us -> 63.4 us
    unnamed x7 -> x0, local copies, waits for them, and re-layouts: 4.19 us -> none
    pallas_call x1 -> x2, Pallas kernels: 66.8 us -> 63.4 us  [the longest x1 61.5 us: local(): pl.pallas_call(functools.partial(kernel, s), out_shape=(pltpu.VMEM((half,...]
where the time goes in v3:
time: 64.2 us; the launch traced here: 64.1 us
  Pallas kernels  63.4 us (99%)
    pallas_call x1, Pallas kernels, local(): pl.pallas_call(functools.partial(kernel, s), out_shape=(pltpu.VMEM((half,...  61.5 us
    pallas_call x1, Pallas kernels, local(): pl.pallas_call(functools.partial(deliver, signals * mb * n_row), out_shap...  1.88 us

profile of v3, /device:TPU:0, one launch (start us, length us, event | category | flops | bytes accessed | tf_op | source)
XLA Modules:
  0.0 64.1 jit_solution(17507502838496292586)
XLA Ops:
  0.6 61.5 %shard_map.58 = (f32[128,4096]{1,0:T(8,128)S(1)}, f32[40,128]{1,0:T(8,128)S(1)}) custom-call(s32[4,1024]{1,0:T(4,128)} %supp_hbm.1, f32[256,512]{1,0:T(8,128)} %meas_hbm.1, bf16[512,4096]{1,0:T(8,128)(2,1)} %a_ref.1), custom_call_target="tpu_custom_call" | custom-call | tf_op jit(solution)/shard_map/pallas_call | solution.py:607
  62.2 1.9 %shard_map.59 = (f32[128,4096]{1,0:T(8,128)}, f32[32,128]{1,0:T(8,128)}, f32[4]{0:T(128)}) custom-call(f32[128,4096]{1,0:T(8,128)S(1)} %get-tuple-element.8.est_ref, f32[40,128]{1,0:T(8,128)S(1)} %get-tuple-element.9.sums_ref), custom_call_target="tpu_custom_call" | custom-call | tf_op jit(solution)/shard_map/pallas_call | solution.py:682

commit v4 on v3

--- a/solution.py
+++ b/solution.py
@@ -11,8 +11,8 @@
 KMAX = 128
 STEP_SIZE = 0.25
 CHUNK = 256
-AHEAD = 896
-LATE = 1
+AHEAD = 768
+LATE = 0
 BF = jnp.bfloat16
 F32 = jnp.float32
 NT = (((1,), (1,)), ((), ()))
@@ -196,8 +196,12 @@
     left_later(part_recv.at[pl.ds(0, 2 * n_row - 1)], part_left)
     part_recv[core] = part_send[core]
 
-    gi = chip // gm
-    gj = lax.rem(chip, gm)
+    def piece_of(j):
+        return (j // gm) * gm + lax.rem(lax.rem(j, gm) + core * gr, gm)
+
+    my_piece = piece_of(chip)
+    gi = my_piece // gm
+    gj = lax.rem(my_piece, gm)
     owner_row = gj // gr
     piece_lane = pl.ds(pl.multiple_of(lax.rem(gj, gr) * pm, 128), pm)
 
@@ -260,12 +264,12 @@
 
     def sum_of(t, h):
         took(rs.at[t, h], rs_sem.at[t, h])
-        return img[t, h, chip].astype(F32) + sum(rs[t, h, k].astype(F32) for k in range(chips - 1))
+        return img[t, h, my_piece if t else chip].astype(F32) + sum(rs[t, h, k].astype(F32) for k in range(chips - 1))
 
     def scatter(t, h):
         for k in range(1, chips):
             put(
-                img.at[t, h, chip_at(k)], rs.at[t, h, k - 1], rs_left.at[t, h], rs_sem.at[t, h],
+                img.at[t, h, piece_of(chip_at(k)) if t else chip_at(k)], rs.at[t, h, k - 1], rs_left.at[t, h], rs_sem.at[t, h],
                 x, chip_at(k) * 2 + core,
             )
         left_later(rs.at[t, h], rs_left.at[t, h])
@@ -348,7 +352,7 @@
 
     def foth_copy(h, k):
         return pltpu.make_async_remote_copy(
-            src_ref=fin.at[core, h, chip], dst_ref=foth.at[jnp.maximum(away - 1, 0), core, h, slot],
+            src_ref=fin.at[core, h, my_piece], dst_ref=foth.at[jnp.maximum(away - 1, 0), core, h, slot],
             send_sem=foth_left.at[h], recv_sem=foth_sem.at[h],
             device_id={"row": owner_row, "col": chip_at(k) * 2 + core}, device_id_type=MESH,
         )
@@ -388,13 +392,13 @@
             residual = mpiece[h] - sum_of(t, h)
             found.append(energy(residual))
             if t < iters - 2:
-                res[t + 1, h, chip] = residual.astype(BF)
-                piece = res.at[t + 1, h, chip]
+                res[t + 1, h, my_piece] = residual.astype(BF)
+                piece = res.at[t + 1, h, my_piece]
                 for k in range(1, chips):
                     put(piece, piece, ag_left.at[t, h], ag_sem.at[t, h], x, chip_at(k) * 2 + core)
                 left_later(rs.at[0, 0], ag_left.at[t, h])
                 continue
-            fin[core, h, chip] = residual.astype(BF)
+            fin[core, h, my_piece] = residual.astype(BF)
 
             @pl.when(away > 0)
             def _():
@@ -404,7 +408,7 @@
             if h == chains - 1:
                 for i in range(early, near):
                     prefetch(i)
-            piece = fin.at[core, h, chip]
+            piece = fin.at[core, h, my_piece]
             for k in range(1, chips):
                 put(piece, piece, fin_left.at[h], fin_sem.at[h], x, chip_at(k) * 2 + core)
             left_later(rs.at[0, 0], fin_left.at[h])
@@ -463,7 +467,7 @@
                 there = slice(at.start - ahead, at.stop - ahead)
                 qsend[d - 1, c, :, there] = nn(theirs, a_vm[:, at]).astype(BF)
                 put(
-                    qsend.at[d - 1, c, :, there], qrecv.at[d - 1, c, :, there], q_left, q_sem.at[d - 1, c, i],
+                    qsend.at[d - 1, c, :, there], qrecv.at[d - 1, c, :, there], q_left, q_sem.at[d - 1, i],
                     row_from(d), col,
                 )
 
@@ -530,8 +534,7 @@
     for i, at in enumerate(spans):
         there = slice(at.start - ahead, at.stop - ahead)
         for d in range(1, n_row):
-            for c in (1, 0):
-                took(qrecv.at[d - 1, c, :, there], q_sem.at[d - 1, c, i])
+            took(qrecv.at[d - 1, :, :, there], q_sem.at[d - 1, i])
         finish(at, sum(
             jnp.concatenate([qrecv[d - 1, c, :, there] for c in range(2)], axis=0).astype(F32)
             for d in range(1, n_row)
@@ -572,7 +575,7 @@
 
 
 def deliver(entries, est_ref, sums_ref, est_out, norm_out, energy_out, sem):
-    parts = 4
+    parts = 8
     rows = est_ref.shape[0] // parts
     lines = norm_out.shape[0]
     copies = [pltpu.make_async_copy(sums_ref.at[pl.ds(0, lines)], norm_out, sem.at[parts])] + [
@@ -670,7 +673,7 @@
             dma((chains,)),
             dma((chains, peers)),
             dma,
-            dma((peers, 2, late)),
+            dma((peers, late)),
             dma,
             dma((2,)),
             dma((2,)),
@@ -691,7 +694,7 @@
             pl.BlockSpec(memory_space=pltpu.HBM), pl.BlockSpec(memory_space=pltpu.HBM),
             pl.BlockSpec(memory_space=pltpu.SMEM),
         ),
-        scratch_shapes=[dma((5,))],
+        scratch_shapes=[dma((9,))],
         compiler_params=pltpu.CompilerParams(vmem_limit_bytes=8 * 1024 * 1024),
     )(*outs)
     return estimate, norms.reshape(columns), energy

time: 64.2 us -> 63.1 us (0.983)
  Pallas kernels: 63.4 us -> 62.4 us
    pallas_call x1, Pallas kernels: 61.5 us -> 60.4 us  [local(): pl.pallas_call(functools.partial(kernel, s), out_shape=(pltpu.VMEM((half,...]
where the time goes in v4:
time: 63.1 us; the launch traced here: 63 us
  Pallas kernels  62.4 us (99%)
  between operations  0.64 us (1%)
    pallas_call x1, Pallas kernels, local(): pl.pallas_call(functools.partial(kernel, s), out_shape=(pltpu.VMEM((half,...  60.4 us
    pallas_call x1, Pallas kernels, local(): pl.pallas_call(functools.partial(deliver, signals * mb * n_row), out_shap...  1.91 us

profile of v4, /device:TPU:0, one launch (start us, length us, event | category | flops | bytes accessed | tf_op | source)
XLA Modules:
  0.0 63.0 jit_solution(7292214529744586088)
XLA Ops:
  0.6 60.4 %shard_map.58 = (f32[128,4096]{1,0:T(8,128)S(1)}, f32[40,128]{1,0:T(8,128)S(1)}) custom-call(s32[4,1024]{1,0:T(4,128)} %supp_hbm.1, f32[256,512]{1,0:T(8,128)} %meas_hbm.1, bf16[512,4096]{1,0:T(8,128)(2,1)} %a_ref.1), custom_call_target="tpu_custom_call" | custom-call | tf_op jit(solution)/shard_map/pallas_call | solution.py:610
  61.1 1.9 %shard_map.59 = (f32[128,4096]{1,0:T(8,128)}, f32[32,128]{1,0:T(8,128)}, f32[4]{0:T(128)}) custom-call(f32[128,4096]{1,0:T(8,128)S(1)} %get-tuple-element.8.est_ref, f32[40,128]{1,0:T(8,128)S(1)} %get-tuple-element.9.sums_ref), custom_call_target="tpu_custom_call" | custom-call | tf_op jit(solution)/shard_map/pallas_call | solution.py:685

commit v5 on v4

--- a/solution.py
+++ b/solution.py
@@ -10,9 +10,9 @@
 MESH = pl.DeviceIdType.MESH
 KMAX = 128
 STEP_SIZE = 0.25
-CHUNK = 256
+CHUNK = 512
 AHEAD = 768
-LATE = 0
+LATE = 2
 BF = jnp.bfloat16
 F32 = jnp.float32
 NT = (((1,), (1,)), ((), ()))
@@ -345,6 +345,12 @@
     relay_kept(1)
     for i in range(early):
         prefetch(i)
+
+    @pl.when(core == 0)
+    def _():
+        for i in range(early, near):
+            prefetch(i)
+
     wait_kept(1)
 
     away = lax.rem(owner_row + n_row - x, n_row)
@@ -406,8 +412,12 @@
                     foth_copy(h, k).start()
 
             if h == chains - 1:
-                for i in range(early, near):
-                    prefetch(i)
+
+                @pl.when(core == 1)
+                def _():
+                    for i in range(early, near):
+                        prefetch(i)
+
             piece = fin.at[core, h, my_piece]
             for k in range(1, chips):
                 put(piece, piece, fin_left.at[h], fin_sem.at[h], x, chip_at(k) * 2 + core)

time: 63.1 us -> 63.2 us (level)
  no operation moved by 1% of the time
where the time goes in v5:
time: 63.2 us; the launch traced here: 63 us
  Pallas kernels  62.4 us (99%)
  between operations  0.64 us (1%)
    pallas_call x1, Pallas kernels, local(): pl.pallas_call(functools.partial(kernel, s), out_shape=(pltpu.VMEM((half,...  60.5 us
    pallas_call x1, Pallas kernels, local(): pl.pallas_call(functools.partial(deliver, signals * mb * n_row), out_shap...  1.91 us

profile of v5, /device:TPU:0, one launch (start us, length us, event | category | flops | bytes accessed | tf_op | source)
XLA Modules:
  0.0 63.0 jit_solution(1661760484838960423)
XLA Ops:
  0.6 60.5 %shard_map.58 = (f32[128,4096]{1,0:T(8,128)S(1)}, f32[40,128]{1,0:T(8,128)S(1)}) custom-call(s32[4,1024]{1,0:T(4,128)} %supp_hbm.1, f32[256,512]{1,0:T(8,128)} %meas_hbm.1, bf16[512,4096]{1,0:T(8,128)(2,1)} %a_ref.1), custom_call_target="tpu_custom_call" | custom-call | tf_op jit(solution)/shard_map/pallas_call | solution.py:620
  61.1 1.9 %shard_map.59 = (f32[128,4096]{1,0:T(8,128)}, f32[32,128]{1,0:T(8,128)}, f32[4]{0:T(128)}) custom-call(f32[128,4096]{1,0:T(8,128)S(1)} %get-tuple-element.8.est_ref, f32[40,128]{1,0:T(8,128)S(1)} %get-tuple-element.9.sums_ref), custom_call_target="tpu_custom_call" | custom-call | tf_op jit(solution)/shard_map/pallas_call | solution.py:695
